TPU v7x, 32 devices: a whole 2x2x4 slice. The times are simulated.
32 devices in a mesh: dp: 16 (over z, y, x), mp: 2 (over core).
Axes of the slice: x: 2, y: 2, z: 4, core: 2. Of those that a mesh axis runs over, the one named last changes fastest.
Arguments:
- inputs: bfloat16 [2048, 1792], P('dp', 'mp'), may hold values from -6 to 6
- cotangent: bfloat16 [2048, 1792], P('dp', 'mp'), may hold values from -6 to 6
- gate_weight: bfloat16 [9472, 1792], P(('mp', 'dp')), may hold values from -0.125 to 0.125
- up_weight: bfloat16 [9472, 1792], P(('mp', 'dp')), may hold values from -0.125 to 0.125
- down_weight: bfloat16 [9472, 1792], P(('mp', 'dp')), may hold values from -0.0625 to 0.0625
Outputs:
- input_grad: bfloat16 [2048, 1792], P('dp', 'mp')
- gate_grad: bfloat16 [9472, 1792], P(('mp', 'dp'))
All inputs are finite; a program needn't handle non-finite values.
Results may differ from a plain program's by a relative error of at most 0.009.
Values may be sent and summed in bfloat16 or wider, within the bound.
A program may use at most 320 MiB of HBM per device.

v0:
```python
import jax
import jax.numpy as jnp
from jax import lax
from jax.sharding import PartitionSpec as P


def tdot(left, right):
    return lax.dot_general(
        left, right, (((0,), (0,)), ((), ())), preferred_element_type=jnp.float32
    )


def rdot(left, right):
    return lax.dot_general(
        left, right, (((1,), (1,)), ((), ())), preferred_element_type=jnp.float32
    )


def per_device(inputs, cotangent, gate_weight, up_weight, down_weight):

    def tokens(block):
        rows = lax.all_gather(block, "dp", axis=0, tiled=True)
        return lax.all_gather(rows, "mp", axis=1, tiled=True)

    full_in = tokens(inputs)
    full_cot = tokens(cotangent)
    gate = rdot(full_in, gate_weight)
    up = rdot(full_in, up_weight)
    dhidden = rdot(full_cot, down_weight)
    sig = jax.nn.sigmoid(gate)
    act = gate * sig
    dup = (dhidden * act).astype(jnp.bfloat16)
    dgate = (dhidden * up * sig * (1.0 + gate * (1.0 - sig))).astype(jnp.bfloat16)
    partial = jnp.dot(dgate, gate_weight, preferred_element_type=jnp.float32)
    partial = partial + jnp.dot(dup, up_weight, preferred_element_type=jnp.float32)
    partial = lax.psum_scatter(partial.astype(jnp.bfloat16), "mp", scatter_dimension=1, tiled=True)
    input_grad = lax.psum_scatter(partial, "dp", scatter_dimension=0, tiled=True)
    gate_grad = tdot(dgate, full_in).astype(jnp.bfloat16)
    return (input_grad, gate_grad)


def solution(mesh):
    placed = (
        P("dp", "mp"),
        P("dp", "mp"),
        P(("mp", "dp"), None),
        P(("mp", "dp"), None),
        P(("mp", "dp"), None),
    )
    return jax.shard_map(
        per_device,
        mesh=mesh,
        in_specs=placed,
        out_specs=(P("dp", "mp"), P(("mp", "dp"), None)),
        check_vma=False,
    )
```

profile of v0, /device:TPU:0, one launch (start us, length us, event | category | flops | bytes accessed | tf_op | source)
XLA Modules:
  0.0 350.5 jit_solution(10456565937666532263)
XLA Ops:
  7.2 0.0 all-gather.5.cloned.1.call-start
  7.2 0.7 all-gather.5.cloned.1.call-update
  7.9 0.0 all-gather.9.cloned.1.call-start
  8.0 0.7 all-gather.9.cloned.1.call-update
  8.7 0.0 all-gather.7.cloned.1.call-start
  8.7 76.4 %all-gather.5.cloned.1.call-done = bf16[2048,896]{1,0:T(8,128)(2,1)} async-done(((bf16[128,896]{1,0:T(8,128)(2,1)}), bf16[2048,896]{1,0:T(8,128)(2,1)}) %all-gather.5.cloned.1.call-update) | async-done | bytes 3670032 | tf_op jit(solution)/shard_map/all_gather | solution.py:22
  85.1 0.0 all-gather.7.cloned.1.call-update
  85.1 0.0 all-gather.11.cloned.1.call-start
  85.2 72.9 %all-gather.9.cloned.1.call-done = bf16[2048,896]{1,0:T(8,128)(2,1)} async-done(((bf16[128,896]{1,0:T(8,128)(2,1)}), bf16[2048,896]{1,0:T(8,128)(2,1)}) %all-gather.9.cloned.1.call-update) | async-done | bytes 3670032 | tf_op jit(solution)/shard_map/all_gather | solution.py:22
  158.1 0.0 reduce-scatter.7.cloned.1.call-start
  158.1 18.3 %all-gather.7.cloned.1.call-done = bf16[2048,1792]{1,0:T(8,128)(2,1)} async-done(((bf16[2048,896]{1,0:T(8,128)(2,1)}), bf16[2048,1792]{1,0:T(8,128)(2,1)}) %all-gather.7.cloned.1.call-update) | async-done | bytes 7340048 | tf_op jit(solution)/shard_map/all_gather | solution.py:23
  176.4 5.7 %fusion.5 = f32[2048,296]{0,1:T(8,128)S(1)} fusion(bf16[2048,1792]{1,0:T(8,128)(2,1)} %all-gather.7.cloned.1.call-done, bf16[296,1792]{1,0:T(8,128)(2,1)} %param.9), kind=kOutput, calls=%fused_computation.10 | convolution fusion | flops 2172649472 | bytes 10825728 | tf_op jit(solution)/shard_map/dot_general | solution.py:14
  182.1 15.1 %all-gather.11.cloned.1.call-done = bf16[2048,1792]{1,0:T(8,128)(2,1)} async-done(((bf16[2048,896]{1,0:T(8,128)(2,1)}), bf16[2048,1792]{1,0:T(8,128)(2,1)}) %all-gather.11.cloned.1.call-update) | async-done | bytes 7340048 | tf_op jit(solution)/shard_map/all_gather | solution.py:23
  197.2 5.6 %fusion.6 = f32[2048,296]{0,1:T(8,128)S(1)} fusion(bf16[2048,1792]{1,0:T(8,128)(2,1)} %all-gather.11.cloned.1.call-done, bf16[296,1792]{1,0:T(8,128)(2,1)S(1)} %copy-done), kind=kOutput, calls=%fused_computation.11 | convolution fusion | flops 2172649472 | bytes 10825728 | tf_op jit(solution)/shard_map/dot_general | solution.py:14
  202.9 2.8 fusion.2
  205.7 7.4 %fusion.7 = f32[2048,1792]{1,0:T(8,128)} fusion(bf16[2048,296]{0,1:T(8,128)(2,1)S(1)} %fusion.2, bf16[296,1792]{1,0:T(8,128)(2,1)S(1)} %copy-done), kind=kOutput, calls=%fused_computation.12 | convolution fusion | flops 2172649472 | bytes 16953344 | tf_op jit(solution)/shard_map/dot_general | solution.py:34
  213.1 9.3 %add_convert_fusion = bf16[2048,1792]{1,0:T(8,128)(2,1)} fusion(f32[2048,1792]{1,0:T(8,128)} %fusion.7, bf16[296,1792]{1,0:T(8,128)(2,1)S(1)} %copy-done.4, f32[2048,296]{0,1:T(8,128)S(1)} %fusion.5, f32[2048,296]{0,1:T(8,128)S(1)} %fusion.6), kind=kOutput, calls=%fused_computation | convolution fusion | flops 2183626752 | bytes 27930624 | tf_op jit(solution)/shard_map/dot_general | solution.py:35
  222.4 10.5 %copy.7 = bf16[2048,1792]{0,1:T(8,128)(2,1)} copy(bf16[2048,1792]{1,0:T(8,128)(2,1)} %add_convert_fusion) | data formatting | bytes 14680064
  232.9 0.0 reduce-scatter.5.cloned.1.call-start
  233.0 17.4 %reduce-scatter.7.cloned.1.call-done = bf16[896,2048]{1,0:T(8,128)(2,1)} async-done(((bf16[1792,2048]{1,0:T(8,128)(2,1)}), bf16[896,2048]{1,0:T(8,128)(2,1)}) %reduce-scatter.7.cloned.1.call-update) | async-done | bytes 3670032
  250.4 6.1 %copy.8 = bf16[2048,896]{1,0:T(8,128)(2,1)} copy(bf16[2048,896]{0,1:T(8,128)(2,1)} %bitcast.14) | data formatting | bytes 7340032
  256.5 1.3 copy-done.3
  257.8 6.5 %convolution_convert_fusion = bf16[296,1792]{1,0:T(8,128)(2,1)} fusion(bf16[2048,296]{0,1:T(8,128)(2,1)S(1)} %copy-done.3, bf16[2048,1792]{1,0:T(8,128)(2,1)} %all-gather.11.cloned.1.call-done), kind=kOutput, calls=%fused_computation.5 | convolution fusion | flops 2173179904 | bytes 9613312 | tf_op jit(solution)/shard_map/dot_general | solution.py:8
  264.3 79.3 %reduce-scatter.5.cloned.1.call-done = bf16[128,896]{1,0:T(8,128)(2,1)} async-done(((bf16[2048,896]{1,0:T(8,128)(2,1)}), bf16[128,896]{1,0:T(8,128)(2,1)}) %reduce-scatter.5.cloned.1.call-update) | async-done | bytes 229392 | tf_op jit(solution)/shard_map/reduce_scatter | solution.py:37
  (14 shorter events, 0.1 us)
Async XLA Ops:
  7.2 190.1 %copy-start = (bf16[296,1792]{1,0:T(8,128)(2,1)S(1)}, bf16[296,1792]{1,0:T(8,128)(2,1)}, u32[]{:S(2)}) copy-start(bf16[296,1792]{1,0:T(8,128)(2,1)} %param.7) | copy-start | bytes 3182596
  7.2 77.9 %all-gather.5.cloned.1.call-start = ((), (), s32[]{:S(2)}) async-start(), calls=%async_computation.2 | async-start | bytes 3899392 | tf_op jit(solution)/shard_map/all_gather | solution.py:22
  7.9 150.2 %all-gather.9.cloned.1.call-start = ((), (), s32[]{:S(2)}) async-start(), calls=%async_computation.4 | async-start | bytes 3899392 | tf_op jit(solution)/shard_map/all_gather | solution.py:22
  8.7 167.7 %all-gather.7.cloned.1.call-start = ((), (), s32[]{:S(2)}) async-start(), calls=%async_computation.3 | async-start | bytes 11010048 | tf_op jit(solution)/shard_map/all_gather | solution.py:23
  85.1 112.1 %all-gather.11.cloned.1.call-start = ((), (), s32[]{:S(2)}) async-start(), calls=%async_computation.5 | async-start | bytes 11010048 | tf_op jit(solution)/shard_map/all_gather | solution.py:23
  158.1 92.3 %reduce-scatter.7.cloned.1.call-start = ((), (), s32[]{:S(2)}) async-start(), calls=%async_computation.7 | async-start | bytes 11010048
  197.2 5.6 %copy-start.4 = (bf16[296,1792]{1,0:T(8,128)(2,1)S(1)}, bf16[296,1792]{1,0:T(8,128)(2,1)}, u32[]{:S(2)}) copy-start(bf16[296,1792]{1,0:T(8,128)(2,1)} %param.8) | copy-start | bytes 3182596
  197.2 5.6 %copy-start.5 = (bf16[2048,1792]{1,0:T(8,128)(2,1)S(1)}, bf16[2048,1792]{1,0:T(8,128)(2,1)}, u32[]{:S(2)}) copy-start(bf16[2048,1792]{1,0:T(8,128)(2,1)} %all-gather.11.cloned.1.call-done) | copy-start | bytes 22020100
  205.7 7.4 %copy-start.2 = (bf16[2048,296]{0,1:T(8,128)(2,1)}, bf16[2048,296]{0,1:T(8,128)(2,1)S(1)}, u32[]{:S(2)}) copy-start(bf16[2048,296]{0,1:T(8,128)(2,1)S(1)} %fusion.2) | copy-start | bytes 3637252
  232.9 110.7 %reduce-scatter.5.cloned.1.call-start = ((), (), s32[]{:S(2)}) async-start(), calls=%async_computation.6 | async-start | bytes 3899392 | tf_op jit(solution)/shard_map/reduce_scatter | solution.py:37
  256.5 1.3 copy-start.3
  257.8 85.9 %copy-start.1 = (bf16[296,1792]{1,0:T(8,128)(2,1)S(1)}, bf16[296,1792]{1,0:T(8,128)(2,1)}, u32[]{:S(2)}) copy-start(bf16[296,1792]{1,0:T(8,128)(2,1)} %param.7) | copy-start | bytes 3182596
Sparse Core Ops, SparseCore 0:
  10.7 74.3 all-gather.4
  87.9 70.1 all-gather.8
  159.6 16.7 all-gather.6
  177.8 19.3 all-gather.10
  233.0 17.3 reduce-scatter.6
  256.6 86.9 reduce-scatter.4
where the time goes:
time: 351 us; the launch traced here: 350 us
  waiting for transfers between devices  281 us (80%)
  matrix products  37.3 us (11%)
  local copies, waits for them, and re-layouts  17.9 us (5%)
  between operations  14.2 us (4%)
    all_gather x2, waiting for transfers between devices, tokens(): rows = lax.all_gather(block, 'dp', axis=0, tiled=True)  149 us
    reduce_scatter x1, waiting for transfers between devices, per_device(): lax.psum_scatter(partial, 'dp', scatter_dimension=0, tiled=True)  79.3 us
    all_gather x2, waiting for transfers between devices, tokens(): return lax.all_gather(rows, 'mp', axis=1, tiled=True)  33.4 us
    unnamed x7, waiting for transfers between devices  18.9 us
    unnamed x14, local copies, waits for them, and re-layouts  17.9 us
    dot_general x3, matrix products, rdot(): lax.dot_general(left, right, (((1,), (1,)), ((), ())), preferred_element_...  14.2 us
    dot_general x1, matrix products, per_device(): jnp.dot(dup, up_weight, preferred_element_type=jnp.float32)  9.27 us
    dot_general x1, matrix products, per_device(): partial = jnp.dot(dgate, gate_weight, preferred_element_type=jnp.float32)  7.38 us
  transfers between devices with their start and end apart: 6, of which 6 were waited for; matrix products, arithmetic and copies ran while one was open for 3% of the time, Pallas kernels for 0%

commit v1 on v0

--- a/solution.py
+++ b/solution.py
@@ -2,6 +2,24 @@
 import jax.numpy as jnp
 from jax import lax
 from jax.sharding import PartitionSpec as P
+
+
+def expand_array_all(dim_at, vector):
+    dev_n = lax.psum(1, "dp")
+    arrivals = tuple(((t, (t + 1) % dev_n) for t in range(dev_n)))
+
+    def assign_spots_up(ready):
+        if len(ready) == dev_n:
+            return ready
+        q_next = assign_spots_up([lax.ppermute(ready[0], "dp", arrivals), *ready])
+        return q_next
+
+    v1 = jnp.roll(
+        jnp.concatenate(assign_spots_up([vector]), axis=dim_at),
+        (lax.axis_index("dp") + 1) * vector.shape[dim_at],
+        axis=dim_at,
+    )
+    return v1
 
 
 def tdot(left, right):
@@ -19,7 +37,7 @@
 def per_device(inputs, cotangent, gate_weight, up_weight, down_weight):
 
     def tokens(block):
-        rows = lax.all_gather(block, "dp", axis=0, tiled=True)
+        rows = expand_array_all(0, block)
         return lax.all_gather(rows, "mp", axis=1, tiled=True)
 
     full_in = tokens(inputs)

time: 351 us -> 510 us (1.45)
  waiting for transfers between devices: 281 us -> 411 us
  other arithmetic: 0 us -> 14.4 us
  local copies, waits for them, and re-layouts: 17.9 us -> 28 us
    ppermute x0 -> x30, waiting for transfers between devices: none -> 307 us  [assign_spots_up(): q_next = assign_spots_up([lax.ppermute(ready[0], 'dp', arrivals), *ready])]
    all_gather x2 -> x0, waiting for transfers between devices: 149 us -> none  [tokens(): rows = lax.all_gather(block, 'dp', axis=0, tiled=True)]
    all_gather x2, waiting for transfers between devices: 33.4 us -> 7.26 us  [tokens(): return lax.all_gather(rows, 'mp', axis=1, tiled=True)]
    concatenate x0 -> x2, other arithmetic: none -> 14.4 us  [expand_array_all(): jnp.roll(jnp.concatenate(assign_spots_up([vector]), axis=dim_at), (lax.ax...]
    unnamed x14 -> x56, local copies, waits for them, and re-layouts: 17.9 us -> 27.9 us
    unnamed x7 -> x5, waiting for transfers between devices: 18.9 us -> 17.5 us
  transfers between devices with their start and end apart: 6 -> 34, of which waited for: 6 -> 33; matrix products, arithmetic and copies ran while one was open for 3% -> 4% of each run, Pallas kernels for 0% -> 0%
where the time goes in v1:
time: 510 us
  waiting for transfers between devices  411 us (81%)
  matrix products  38.4 us (8%)
  local copies, waits for them, and re-layouts  28 us (5%)
  other arithmetic  14.4 us (3%)
  between operations  14.1 us (3%)
    ppermute x30, waiting for transfers between devices, assign_spots_up(): q_next = assign_spots_up([lax.ppermute(ready[0], 'dp', arrivals), *ready])  307 us
    reduce_scatter x1, waiting for transfers between devices, per_device(): lax.psum_scatter(partial, 'dp', scatter_dimension=0, tiled=True)  79.4 us
    unnamed x56, local copies, waits for them, and re-layouts  27.9 us
    unnamed x5, waiting for transfers between devices  17.5 us
    dot_general x3, matrix products, rdot(): lax.dot_general(left, right, (((1,), (1,)), ((), ())), preferred_element_...  15.1 us
    concatenate x2, other arithmetic, expand_array_all(): jnp.roll(jnp.concatenate(assign_spots_up([vector]), axis=dim_at), (lax.ax...  14.4 us
  transfers between devices with their start and end apart: 34, of which 33 were waited for; matrix products, arithmetic and copies ran while one was open for 4% of the time, Pallas kernels for 0%

profile of v1, /device:TPU:0, one launch (start us, length us, event | category | flops | bytes accessed | tf_op | source)
XLA Modules:
  0.0 509.7 jit_solution(5478497158257263812)
XLA Ops:
  10.3 9.8 %collective-permute-done = bf16[128,896]{1,0:T(8,128)(2,1)S(1)} collective-permute-done((bf16[128,896]{1,0:T(8,128)(2,1)}, bf16[128,896]{1,0:T(8,128)(2,1)S(1)}, u32[]{:S(2)}, u32[]{:S(2)}) %collective-permute-start) | collective-permute-done | bytes 229408 | tf_op jit(solution)/shard_map/ppermute | solution.py:14
  20.1 10.4 %collective-permute-done.1 = bf16[128,896]{1,0:T(8,128)(2,1)S(1)} collective-permute-done((bf16[128,896]{1,0:T(8,128)(2,1)S(1)}, bf16[128,896]{1,0:T(8,128)(2,1)S(1)}, u32[]{:S(2)}, u32[]{:S(2)}) %collective-permute-start.1) | collective-permute-done | bytes 229408 | tf_op jit(solution)/shard_map/ppermute | solution.py:14
  30.4 9.6 %collective-permute-done.2 = bf16[128,896]{1,0:T(8,128)(2,1)S(1)} collective-permute-done((bf16[128,896]{1,0:T(8,128)(2,1)S(1)}, bf16[128,896]{1,0:T(8,128)(2,1)S(1)}, u32[]{:S(2)}, u32[]{:S(2)}) %collective-permute-start.2) | collective-permute-done | bytes 229408 | tf_op jit(solution)/shard_map/ppermute | solution.py:14
  40.0 9.6 %collective-permute-done.3 = bf16[128,896]{1,0:T(8,128)(2,1)S(1)} collective-permute-done((bf16[128,896]{1,0:T(8,128)(2,1)S(1)}, bf16[128,896]{1,0:T(8,128)(2,1)S(1)}, u32[]{:S(2)}, u32[]{:S(2)}) %collective-permute-start.3) | collective-permute-done | bytes 229408 | tf_op jit(solution)/shard_map/ppermute | solution.py:14
  68.9 10.8 %collective-permute-done.6 = bf16[128,896]{1,0:T(8,128)(2,1)S(1)} collective-permute-done((bf16[128,896]{1,0:T(8,128)(2,1)S(1)}, bf16[128,896]{1,0:T(8,128)(2,1)S(1)}, u32[]{:S(2)}, u32[]{:S(2)}) %collective-permute-start.6) | collective-permute-done | bytes 229408 | tf_op jit(solution)/shard_map/ppermute | solution.py:14
  79.7 11.9 %collective-permute-done.7 = bf16[128,896]{1,0:T(8,128)(2,1)S(1)} collective-permute-done((bf16[128,896]{1,0:T(8,128)(2,1)S(1)}, bf16[128,896]{1,0:T(8,128)(2,1)S(1)}, u32[]{:S(2)}, u32[]{:S(2)}) %collective-permute-start.7) | collective-permute-done | bytes 229408 | tf_op jit(solution)/shard_map/ppermute | solution.py:14
  91.6 11.2 %collective-permute-done.8 = bf16[128,896]{1,0:T(8,128)(2,1)S(1)} collective-permute-done((bf16[128,896]{1,0:T(8,128)(2,1)S(1)}, bf16[128,896]{1,0:T(8,128)(2,1)S(1)}, u32[]{:S(2)}, u32[]{:S(2)}) %collective-permute-start.8) | collective-permute-done | bytes 229408 | tf_op jit(solution)/shard_map/ppermute | solution.py:14
  102.8 11.1 %collective-permute-done.9 = bf16[128,896]{1,0:T(8,128)(2,1)S(1)} collective-permute-done((bf16[128,896]{1,0:T(8,128)(2,1)S(1)}, bf16[128,896]{1,0:T(8,128)(2,1)S(1)}, u32[]{:S(2)}, u32[]{:S(2)}) %collective-permute-start.9) | collective-permute-done | bytes 229408 | tf_op jit(solution)/shard_map/ppermute | solution.py:14
  114.6 10.2 %collective-permute-done.10 = bf16[128,896]{1,0:T(8,128)(2,1)S(1)} collective-permute-done((bf16[128,896]{1,0:T(8,128)(2,1)S(1)}, bf16[128,896]{1,0:T(8,128)(2,1)S(1)}, u32[]{:S(2)}, u32[]{:S(2)}) %collective-permute-start.10) | collective-permute-done | bytes 229408 | tf_op jit(solution)/shard_map/ppermute | solution.py:14
  146.1 9.7 %collective-permute-done.13 = bf16[128,896]{1,0:T(8,128)(2,1)} collective-permute-done((bf16[128,896]{1,0:T(8,128)(2,1)S(1)}, bf16[128,896]{1,0:T(8,128)(2,1)}, u32[]{:S(2)}, u32[]{:S(2)}) %collective-permute-start.13) | collective-permute-done | bytes 229408 | tf_op jit(solution)/shard_map/ppermute | solution.py:14
  155.8 9.9 %collective-permute-done.14 = bf16[128,896]{1,0:T(8,128)(2,1)} collective-permute-done((bf16[128,896]{1,0:T(8,128)(2,1)}, bf16[128,896]{1,0:T(8,128)(2,1)}, u32[]{:S(2)}, u32[]{:S(2)}) %collective-permute-start.14) | collective-permute-done | bytes 229408 | tf_op jit(solution)/shard_map/ppermute | solution.py:14
  180.1 11.6 %collective-permute-done.15 = bf16[128,896]{1,0:T(8,128)(2,1)S(1)} collective-permute-done((bf16[128,896]{1,0:T(8,128)(2,1)S(1)}, bf16[128,896]{1,0:T(8,128)(2,1)S(1)}, u32[]{:S(2)}, u32[]{:S(2)}) %collective-permute-start.15) | collective-permute-done | bytes 229408 | tf_op jit(solution)/shard_map/ppermute | solution.py:14
  191.7 11.4 %collective-permute-done.16 = bf16[128,896]{1,0:T(8,128)(2,1)S(1)} collective-permute-done((bf16[128,896]{1,0:T(8,128)(2,1)S(1)}, bf16[128,896]{1,0:T(8,128)(2,1)S(1)}, u32[]{:S(2)}, u32[]{:S(2)}) %collective-permute-start.16) | collective-permute-done | bytes 229408 | tf_op jit(solution)/shard_map/ppermute | solution.py:14
  203.1 10.5 %collective-permute-done.17 = bf16[128,896]{1,0:T(8,128)(2,1)S(1)} collective-permute-done((bf16[128,896]{1,0:T(8,128)(2,1)S(1)}, bf16[128,896]{1,0:T(8,128)(2,1)S(1)}, u32[]{:S(2)}, u32[]{:S(2)}) %collective-permute-start.17) | collective-permute-done | bytes 229408 | tf_op jit(solution)/shard_map/ppermute | solution.py:14
  213.6 9.7 %collective-permute-done.18 = bf16[128,896]{1,0:T(8,128)(2,1)S(1)} collective-permute-done((bf16[128,896]{1,0:T(8,128)(2,1)S(1)}, bf16[128,896]{1,0:T(8,128)(2,1)S(1)}, u32[]{:S(2)}, u32[]{:S(2)}) %collective-permute-start.18) | collective-permute-done | bytes 229408 | tf_op jit(solution)/shard_map/ppermute | solution.py:14
  223.2 9.6 %collective-permute-done.19 = bf16[128,896]{1,0:T(8,128)(2,1)S(1)} collective-permute-done((bf16[128,896]{1,0:T(8,128)(2,1)S(1)}, bf16[128,896]{1,0:T(8,128)(2,1)S(1)}, u32[]{:S(2)}, u32[]{:S(2)}) %collective-permute-start.19) | collective-permute-done | bytes 229408 | tf_op jit(solution)/shard_map/ppermute | solution.py:14
  252.1 10.3 %collective-permute-done.22 = bf16[128,896]{1,0:T(8,128)(2,1)S(1)} collective-permute-done((bf16[128,896]{1,0:T(8,128)(2,1)S(1)}, bf16[128,896]{1,0:T(8,128)(2,1)S(1)}, u32[]{:S(2)}, u32[]{:S(2)}) %collective-permute-start.22) | collective-permute-done | bytes 229408 | tf_op jit(solution)/shard_map/ppermute | solution.py:14
  262.4 11.5 %collective-permute-done.23 = bf16[128,896]{1,0:T(8,128)(2,1)S(1)} collective-permute-done((bf16[128,896]{1,0:T(8,128)(2,1)S(1)}, bf16[128,896]{1,0:T(8,128)(2,1)S(1)}, u32[]{:S(2)}, u32[]{:S(2)}) %collective-permute-start.23) | collective-permute-done | bytes 229408 | tf_op jit(solution)/shard_map/ppermute | solution.py:14
  273.9 11.5 %collective-permute-done.24 = bf16[128,896]{1,0:T(8,128)(2,1)S(1)} collective-permute-done((bf16[128,896]{1,0:T(8,128)(2,1)S(1)}, bf16[128,896]{1,0:T(8,128)(2,1)S(1)}, u32[]{:S(2)}, u32[]{:S(2)}) %collective-permute-start.24) | collective-permute-done | bytes 229408 | tf_op jit(solution)/shard_map/ppermute | solution.py:14
  285.4 10.7 %collective-permute-done.25 = bf16[128,896]{1,0:T(8,128)(2,1)S(1)} collective-permute-done((bf16[128,896]{1,0:T(8,128)(2,1)S(1)}, bf16[128,896]{1,0:T(8,128)(2,1)S(1)}, u32[]{:S(2)}, u32[]{:S(2)}) %collective-permute-start.25) | collective-permute-done | bytes 229408 | tf_op jit(solution)/shard_map/ppermute | solution.py:14
  296.1 9.8 %collective-permute-done.26 = bf16[128,896]{1,0:T(8,128)(2,1)S(1)} collective-permute-done((bf16[128,896]{1,0:T(8,128)(2,1)S(1)}, bf16[128,896]{1,0:T(8,128)(2,1)S(1)}, u32[]{:S(2)}, u32[]{:S(2)}) %collective-permute-start.26) | collective-permute-done | bytes 229408 | tf_op jit(solution)/shard_map/ppermute | solution.py:14
  382.0 10.5 %copy.7 = bf16[2048,1792]{0,1:T(8,128)(2,1)} copy(bf16[2048,1792]{1,0:T(8,128)(2,1)} %add_convert_fusion) | data formatting | bytes 14680064
  392.6 17.4 %reduce-scatter.7.cloned.1.call-done = bf16[896,2048]{1,0:T(8,128)(2,1)} async-done(((bf16[1792,2048]{1,0:T(8,128)(2,1)}), bf16[896,2048]{1,0:T(8,128)(2,1)}) %reduce-scatter.7.cloned.1.call-update) | async-done | bytes 3670032
  423.9 79.4 %reduce-scatter.5.cloned.1.call-done = bf16[128,896]{1,0:T(8,128)(2,1)} async-done(((bf16[2048,896]{1,0:T(8,128)(2,1)}), bf16[128,896]{1,0:T(8,128)(2,1)}) %reduce-scatter.5.cloned.1.call-update) | async-done | bytes 229392 | tf_op jit(solution)/shard_map/reduce_scatter | solution.py:55
  (114 shorter events, 167.6 us)
Async XLA Ops:
  7.2 335.6 %all-gather.3.cloned.1.call-start = ((), (), s32[]{:S(2)}) async-start(), calls=%async_computation.2 | async-start | bytes 11010048 | tf_op jit(solution)/shard_map/all_gather | solution.py:41
  7.2 12.8 %collective-permute-start = (bf16[128,896]{1,0:T(8,128)(2,1)}, bf16[128,896]{1,0:T(8,128)(2,1)S(1)}, u32[]{:S(2)}, u32[]{:S(2)}) collective-permute-start(bf16[128,896]{1,0:T(8,128)(2,1)} %param.8), channel_id=1, source_target_pairs={{0,2},{2,4},{4,6},{6,8},{8,10},{10,12},{12,14},{14,16},{16,18},{18... | collective-permute-start | bytes 688136 | tf_op jit(solution)/shard_map/ppermute | solution.py:14
  20.1 10.4 %collective-permute-start.1 = (bf16[128,896]{1,0:T(8,128)(2,1)S(1)}, bf16[128,896]{1,0:T(8,128)(2,1)S(1)}, u32[]{:S(2)}, u32[]{:S(2)}) collective-permute-start(bf16[128,896]{1,0:T(8,128)(2,1)S(1)} %collective-permute-done), channel_id=1, source_target_pairs={{0,2},{2,4},{4,6},{6,8},{8,10},{10,12},{12,14},{14,16},{16,18},{18... | collective-permute-start | bytes 688136 | tf_op jit(solution)/shard_map/ppermute | solution.py:14
  30.4 9.6 %collective-permute-start.2 = (bf16[128,896]{1,0:T(8,128)(2,1)S(1)}, bf16[128,896]{1,0:T(8,128)(2,1)S(1)}, u32[]{:S(2)}, u32[]{:S(2)}) collective-permute-start(bf16[128,896]{1,0:T(8,128)(2,1)S(1)} %collective-permute-done.1), channel_id=1, source_target_pairs={{0,2},{2,4},{4,6},{6,8},{8,10},{10,12},{12,14},{14,16},{16,18},{18... | collective-permute-start | bytes 688136 | tf_op jit(solution)/shard_map/ppermute | solution.py:14
  68.9 10.8 %collective-permute-start.6 = (bf16[128,896]{1,0:T(8,128)(2,1)S(1)}, bf16[128,896]{1,0:T(8,128)(2,1)S(1)}, u32[]{:S(2)}, u32[]{:S(2)}) collective-permute-start(bf16[128,896]{1,0:T(8,128)(2,1)S(1)} %collective-permute-done.5), channel_id=1, source_target_pairs={{0,2},{2,4},{4,6},{6,8},{8,10},{10,12},{12,14},{14,16},{16,18},{18... | collective-permute-start | bytes 688136 | tf_op jit(solution)/shard_map/ppermute | solution.py:14
  79.7 11.9 %collective-permute-start.7 = (bf16[128,896]{1,0:T(8,128)(2,1)S(1)}, bf16[128,896]{1,0:T(8,128)(2,1)S(1)}, u32[]{:S(2)}, u32[]{:S(2)}) collective-permute-start(bf16[128,896]{1,0:T(8,128)(2,1)S(1)} %collective-permute-done.6), channel_id=1, source_target_pairs={{0,2},{2,4},{4,6},{6,8},{8,10},{10,12},{12,14},{14,16},{16,18},{18... | collective-permute-start | bytes 688136 | tf_op jit(solution)/shard_map/ppermute | solution.py:14
  91.6 11.2 %collective-permute-start.8 = (bf16[128,896]{1,0:T(8,128)(2,1)S(1)}, bf16[128,896]{1,0:T(8,128)(2,1)S(1)}, u32[]{:S(2)}, u32[]{:S(2)}) collective-permute-start(bf16[128,896]{1,0:T(8,128)(2,1)S(1)} %collective-permute-done.7), channel_id=1, source_target_pairs={{0,2},{2,4},{4,6},{6,8},{8,10},{10,12},{12,14},{14,16},{16,18},{18... | collective-permute-start | bytes 688136 | tf_op jit(solution)/shard_map/ppermute | solution.py:14
  102.8 11.1 %collective-permute-start.9 = (bf16[128,896]{1,0:T(8,128)(2,1)S(1)}, bf16[128,896]{1,0:T(8,128)(2,1)S(1)}, u32[]{:S(2)}, u32[]{:S(2)}) collective-permute-start(bf16[128,896]{1,0:T(8,128)(2,1)S(1)} %collective-permute-done.8), channel_id=1, source_target_pairs={{0,2},{2,4},{4,6},{6,8},{8,10},{10,12},{12,14},{14,16},{16,18},{18... | collective-permute-start | bytes 688136 | tf_op jit(solution)/shard_map/ppermute | solution.py:14
  114.6 10.2 %collective-permute-start.10 = (bf16[128,896]{1,0:T(8,128)(2,1)S(1)}, bf16[128,896]{1,0:T(8,128)(2,1)S(1)}, u32[]{:S(2)}, u32[]{:S(2)}) collective-permute-start(bf16[128,896]{1,0:T(8,128)(2,1)S(1)} %collective-permute-done.9), channel_id=1, source_target_pairs={{0,2},{2,4},{4,6},{6,8},{8,10},{10,12},{12,14},{14,16},{16,18},{18... | collective-permute-start | bytes 688136 | tf_op jit(solution)/shard_map/ppermute | solution.py:14
  146.1 9.7 %collective-permute-start.13 = (bf16[128,896]{1,0:T(8,128)(2,1)S(1)}, bf16[128,896]{1,0:T(8,128)(2,1)}, u32[]{:S(2)}, u32[]{:S(2)}) collective-permute-start(bf16[128,896]{1,0:T(8,128)(2,1)S(1)} %collective-permute-done.12), channel_id=1, source_target_pairs={{0,2},{2,4},{4,6},{6,8},{8,10},{10,12},{12,14},{14,16},{16,18},{18... | collective-permute-start | bytes 688136 | tf_op jit(solution)/shard_map/ppermute | solution.py:14
  155.8 9.9 %collective-permute-start.14 = (bf16[128,896]{1,0:T(8,128)(2,1)}, bf16[128,896]{1,0:T(8,128)(2,1)}, u32[]{:S(2)}, u32[]{:S(2)}) collective-permute-start(bf16[128,896]{1,0:T(8,128)(2,1)} %collective-permute-done.13), channel_id=1, source_target_pairs={{0,2},{2,4},{4,6},{6,8},{8,10},{10,12},{12,14},{14,16},{16,18},{18... | collective-permute-start | bytes 688136 | tf_op jit(solution)/shard_map/ppermute | solution.py:14
  179.1 177.6 %all-gather.5.cloned.1.call-start = ((), (), s32[]{:S(2)}) async-start(), calls=%async_computation.3 | async-start | bytes 11010048 | tf_op jit(solution)/shard_map/all_gather | solution.py:41
  180.0 11.6 %collective-permute-start.15 = (bf16[128,896]{1,0:T(8,128)(2,1)S(1)}, bf16[128,896]{1,0:T(8,128)(2,1)S(1)}, u32[]{:S(2)}, u32[]{:S(2)}) collective-permute-start(bf16[128,896]{1,0:T(8,128)(2,1)S(1)} %copy-done.6), channel_id=1, source_target_pairs={{0,2},{2,4},{4,6},{6,8},{8,10},{10,12},{12,14},{14,16},{16,18},{18... | collective-permute-start | bytes 688136 | tf_op jit(solution)/shard_map/ppermute | solution.py:14
  191.7 11.4 %collective-permute-start.16 = (bf16[128,896]{1,0:T(8,128)(2,1)S(1)}, bf16[128,896]{1,0:T(8,128)(2,1)S(1)}, u32[]{:S(2)}, u32[]{:S(2)}) collective-permute-start(bf16[128,896]{1,0:T(8,128)(2,1)S(1)} %collective-permute-done.15), channel_id=1, source_target_pairs={{0,2},{2,4},{4,6},{6,8},{8,10},{10,12},{12,14},{14,16},{16,18},{18... | collective-permute-start | bytes 688136 | tf_op jit(solution)/shard_map/ppermute | solution.py:14
  203.0 10.5 %collective-permute-start.17 = (bf16[128,896]{1,0:T(8,128)(2,1)S(1)}, bf16[128,896]{1,0:T(8,128)(2,1)S(1)}, u32[]{:S(2)}, u32[]{:S(2)}) collective-permute-start(bf16[128,896]{1,0:T(8,128)(2,1)S(1)} %collective-permute-done.16), channel_id=1, source_target_pairs={{0,2},{2,4},{4,6},{6,8},{8,10},{10,12},{12,14},{14,16},{16,18},{18... | collective-permute-start | bytes 688136 | tf_op jit(solution)/shard_map/ppermute | solution.py:14
  213.6 9.7 %collective-permute-start.18 = (bf16[128,896]{1,0:T(8,128)(2,1)S(1)}, bf16[128,896]{1,0:T(8,128)(2,1)S(1)}, u32[]{:S(2)}, u32[]{:S(2)}) collective-permute-start(bf16[128,896]{1,0:T(8,128)(2,1)S(1)} %collective-permute-done.17), channel_id=1, source_target_pairs={{0,2},{2,4},{4,6},{6,8},{8,10},{10,12},{12,14},{14,16},{16,18},{18... | collective-permute-start | bytes 688136 | tf_op jit(solution)/shard_map/ppermute | solution.py:14
  252.1 10.3 %collective-permute-start.22 = (bf16[128,896]{1,0:T(8,128)(2,1)S(1)}, bf16[128,896]{1,0:T(8,128)(2,1)S(1)}, u32[]{:S(2)}, u32[]{:S(2)}) collective-permute-start(bf16[128,896]{1,0:T(8,128)(2,1)S(1)} %collective-permute-done.21), channel_id=1, source_target_pairs={{0,2},{2,4},{4,6},{6,8},{8,10},{10,12},{12,14},{14,16},{16,18},{18... | collective-permute-start | bytes 688136 | tf_op jit(solution)/shard_map/ppermute | solution.py:14
  262.4 11.5 %collective-permute-start.23 = (bf16[128,896]{1,0:T(8,128)(2,1)S(1)}, bf16[128,896]{1,0:T(8,128)(2,1)S(1)}, u32[]{:S(2)}, u32[]{:S(2)}) collective-permute-start(bf16[128,896]{1,0:T(8,128)(2,1)S(1)} %collective-permute-done.22), channel_id=1, source_target_pairs={{0,2},{2,4},{4,6},{6,8},{8,10},{10,12},{12,14},{14,16},{16,18},{18... | collective-permute-start | bytes 688136 | tf_op jit(solution)/shard_map/ppermute | solution.py:14
  273.9 11.5 %collective-permute-start.24 = (bf16[128,896]{1,0:T(8,128)(2,1)S(1)}, bf16[128,896]{1,0:T(8,128)(2,1)S(1)}, u32[]{:S(2)}, u32[]{:S(2)}) collective-permute-start(bf16[128,896]{1,0:T(8,128)(2,1)S(1)} %collective-permute-done.23), channel_id=1, source_target_pairs={{0,2},{2,4},{4,6},{6,8},{8,10},{10,12},{12,14},{14,16},{16,18},{18... | collective-permute-start | bytes 688136 | tf_op jit(solution)/shard_map/ppermute | solution.py:14
  285.4 10.7 %collective-permute-start.25 = (bf16[128,896]{1,0:T(8,128)(2,1)S(1)}, bf16[128,896]{1,0:T(8,128)(2,1)S(1)}, u32[]{:S(2)}, u32[]{:S(2)}) collective-permute-start(bf16[128,896]{1,0:T(8,128)(2,1)S(1)} %collective-permute-done.24), channel_id=1, source_target_pairs={{0,2},{2,4},{4,6},{6,8},{8,10},{10,12},{12,14},{14,16},{16,18},{18... | collective-permute-start | bytes 688136 | tf_op jit(solution)/shard_map/ppermute | solution.py:14
  296.1 9.8 %collective-permute-start.26 = (bf16[128,896]{1,0:T(8,128)(2,1)S(1)}, bf16[128,896]{1,0:T(8,128)(2,1)S(1)}, u32[]{:S(2)}, u32[]{:S(2)}) collective-permute-start(bf16[128,896]{1,0:T(8,128)(2,1)S(1)} %collective-permute-done.25), channel_id=1, source_target_pairs={{0,2},{2,4},{4,6},{6,8},{8,10},{10,12},{12,14},{14,16},{16,18},{18... | collective-permute-start | bytes 688136 | tf_op jit(solution)/shard_map/ppermute | solution.py:14
  325.1 9.6 %collective-permute-start.29 = (bf16[128,896]{1,0:T(8,128)(2,1)S(1)}, bf16[128,896]{1,0:T(8,128)(2,1)S(1)}, u32[]{:S(2)}, u32[]{:S(2)}) collective-permute-start(bf16[128,896]{1,0:T(8,128)(2,1)S(1)} %collective-permute-done.28), channel_id=1, source_target_pairs={{0,2},{2,4},{4,6},{6,8},{8,10},{10,12},{12,14},{14,16},{16,18},{18... | collective-permute-start | bytes 688136 | tf_op jit(solution)/shard_map/ppermute | solution.py:14
  342.5 67.5 %reduce-scatter.7.cloned.1.call-start = ((), (), s32[]{:S(2)}) async-start(), calls=%async_computation.5 | async-start | bytes 11010048
  392.5 110.7 %reduce-scatter.5.cloned.1.call-start = ((), (), s32[]{:S(2)}) async-start(), calls=%async_computation.4 | async-start | bytes 3899392 | tf_op jit(solution)/shard_map/reduce_scatter | solution.py:55
  (22 other events, 720.0 us)
Sparse Core Ops, SparseCore 0:
  179.3 14.0 all-gather.2
  342.6 14.0 all-gather.4
  392.6 17.3 reduce-scatter.6
  416.2 86.9 reduce-scatter.4
